TPU v7x, 32 devices: a whole 2x2x4 slice. The times are simulated.
32 devices in a mesh: segment: 8 (over z, x), dp: 4 (over y, core).
Axes of the slice: x: 2, y: 2, z: 4, core: 2. Of those that a mesh axis runs over, the one named last changes fastest.
Arguments:
- src_embed: bfloat16 [16, 128, 2048], P('dp', None, 'segment'), parts along dimension 0, may hold values from -6 to 6
- tgt_embed: bfloat16 [16, 128, 2048], P('dp', None, 'segment'), parts along dimension 0, may hold values from -6 to 6
- src_lengths: int32 [16], P('dp'), parts along dimension 0, may hold values from 32 to 128
- tgt_lengths: int32 [16], P('dp'), parts along dimension 0, may hold values from 32 to 128
- attn_in: bfloat16 [8, 2048, 3072], P('segment'), may hold values from -0.125 to 0.125
- attn_out: bfloat16 [8, 1024, 2048], P('segment'), may hold values from -0.375 to 0.375
- norm_gain: float32 [4, 2048], replicated, may hold values from 0.25 to 1.75
- final_gain: float32 [2048], replicated, may hold values from 0.25 to 1.75
Outputs:
- decoded: bfloat16 [16, 128, 2048], P('dp', None, 'segment'), parts along dimension 0
There are 4 independent parts, one for each index of `dp`. A program takes and returns all parts, laid end to end along the dimension named above; an argument that names none is the same for every part. Nothing has to cross between parts.
Inputs may be any that keep to these rules, and one draw needn't show every extreme that they name: `src_lengths`: keys at positions below a sequence's length are its real tokens. `tgt_lengths`: keys at positions below a sequence's length are its real tokens.
All inputs are finite; a program needn't handle non-finite values.
Results may differ from a plain program's by a relative error of at most 0.015.
Values may be sent and summed in bfloat16 or wider, within the bound.
A program may use at most 64 MiB of HBM per device.

v0:
```python
import jax
import jax.numpy as jnp
from jax import lax
from jax.sharding import PartitionSpec as P

HEAD = 64
epsilon = 1e-06
score_scale = 0.125


def partner(value, axis, distance):
    mask = 2**distance
    pairs = [(source, source ^ mask) for source in range(lax.axis_size(axis))]
    return lax.ppermute(value, axis, pairs)


def shifted(value, axis, by):
    length = lax.axis_size(axis)
    pairs = [(i, i + by) for i in range(length) if 0 <= i + by < length]
    return lax.ppermute(value, axis, pairs)


def rms_scale(values, gain_vector):
    return (
        values
        * lax.rsqrt(jnp.mean(values * values, axis=-1, keepdims=True) + epsilon)
        * gain_vector
    )


def attention(queries, key_rows, values, allowed):
    head_count = queries.shape[1] // HEAD
    shaped_q = queries.reshape(queries.shape[0], head_count, HEAD)
    shaped_k = key_rows.reshape(key_rows.shape[0], head_count, HEAD)
    shaped_v = values.reshape(values.shape[0], head_count, HEAD)
    scores = (
        jnp.einsum("qhd,khd->hqk", shaped_q, shaped_k, preferred_element_type=jnp.float32)
        * score_scale
    )
    scores = jnp.where(allowed[None], scores, -1000000000.0)
    weights = jax.nn.softmax(scores, axis=-1).astype(jnp.bfloat16)
    mixture = jnp.einsum("hqk,khd->qhd", weights, shaped_v, preferred_element_type=jnp.float32)
    return mixture.reshape(queries.shape[0], -1).astype(jnp.bfloat16)


def pick_row(array, row_slot):
    return lax.dynamic_index_in_dim(array, row_slot, 0, keepdims=False)


def place_row(array, row_slot, update, keep_flag):
    former = pick_row(array, row_slot)
    return lax.dynamic_update_index_in_dim(array, jnp.where(keep_flag, update, former), row_slot, 0)


def on_device(
    src_embed, tgt_embed, src_lengths, tgt_lengths, attn_in, attn_out, norm_gain, final_gain
):
    segments = lax.axis_size("segment")
    group_size = segments // 4
    bit_count = group_size.bit_length() - 1
    segment_index = lax.axis_index("segment")
    section = segment_index // group_size
    member = segment_index % group_size
    batches, seq_len, column_share = src_embed.shape
    full_width = column_share * segments
    destination = (jnp.arange(segments, dtype=jnp.int32) // group_size)[None, None, :, None]
    outgoing = jnp.where(
        destination == 0,
        src_embed[:, :, None, :],
        jnp.where(destination == 2, tgt_embed[:, :, None, :], jnp.zeros((), jnp.bfloat16)),
    )
    arrived = lax.all_to_all(outgoing, "segment", split_axis=2, concat_axis=2, tiled=True)
    embedded = arrived.reshape(batches, seq_len, full_width)
    in_weight = attn_in[0]
    out_weight = attn_out[0]
    head_cols = out_weight.shape[0]
    layer_gain = pick_row(norm_gain, section)
    positions = jnp.arange(seq_len, dtype=jnp.int32)
    causal = positions[None, :] <= positions[:, None]
    is_target = section == 3
    starts_chain = (section == 0) | (section == 2)

    def allowed_for(batch_slot):
        seq_length = jnp.where(
            is_target, pick_row(tgt_lengths, batch_slot), pick_row(src_lengths, batch_slot)
        )
        return (positions[None, :] < seq_length) & (causal | jnp.logical_not(is_target))

    def head_partial(current, memory, batch_slot):
        normed = rms_scale(current.astype(jnp.float32), layer_gain).astype(jnp.bfloat16)
        source = jnp.where(section == 2, memory, normed)
        queries = jnp.dot(
            normed, in_weight[:, :head_cols], preferred_element_type=jnp.float32
        ).astype(jnp.bfloat16)
        key_value = jnp.dot(
            source, in_weight[:, head_cols:], preferred_element_type=jnp.float32
        ).astype(jnp.bfloat16)
        mixture = attention(
            queries, key_value[:, :head_cols], key_value[:, head_cols:], allowed_for(batch_slot)
        )
        return jnp.dot(mixture, out_weight, preferred_element_type=jnp.float32)

    def combine_heads(current, partial_sum):
        summed = partial_sum
        for bit_index in range(bit_count):
            summed = summed + partner(summed, "segment", bit_index)
        return (current.astype(jnp.float32) + summed).astype(jnp.bfloat16)

    def final_norm(output):
        return rms_scale(output.astype(jnp.float32), final_gain).astype(jnp.bfloat16)

    zero_sum = jnp.zeros((seq_len, full_width), jnp.float32)

    def run_sublayer(step_index, received):
        slot_raw = step_index - section
        active = (slot_raw >= 0) & (slot_raw < batches)
        batch_slot = jnp.clip(slot_raw, 0, batches - 1)
        current = jnp.where(starts_chain, pick_row(embedded, batch_slot), received)
        partial_sum = lax.cond(
            active,
            lambda value_in, memory_in: head_partial(value_in, memory_in, batch_slot),
            lambda value_in, memory_in: zero_sum,
            current,
            received,
        )
        output = combine_heads(current, partial_sum)
        return (output, batch_slot, active)

    empty_rows = jnp.zeros((seq_len, full_width), jnp.bfloat16)
    collected = jnp.zeros((batches, seq_len, full_width), jnp.bfloat16)

    def relay_step(step_index, state_tuple):
        received, outputs = state_tuple
        output, batch_slot, active = run_sublayer(step_index, received)
        outputs = place_row(outputs, batch_slot, output, active & (section == 3))
        leaving = jnp.where(section == 1, final_norm(output), output)
        forwarded = shifted(leaving, "segment", group_size)
        return (forwarded, outputs)

    state_tuple = lax.fori_loop(0, batches + 3, relay_step, (empty_rows, collected))
    outputs = state_tuple[1]
    decoded_cols = lax.dynamic_slice_in_dim(outputs, segment_index * column_share, column_share, 2)
    for distance in range(1, 4):
        chosen = lax.dynamic_slice_in_dim(
            outputs, ((3 - distance) * group_size + member) * column_share, column_share, 2
        )
        incoming = shifted(chosen, "segment", -distance * group_size)
        decoded_cols = jnp.where(section == 3 - distance, incoming, decoded_cols)
    return decoded_cols


def solution(mesh):
    in_specs = (
        P("dp", None, "segment"),
        P("dp", None, "segment"),
        P("dp"),
        P("dp"),
        P("segment", None, None),
        P("segment", None, None),
        P(),
        P(),
    )
    out_specs = P("dp", None, "segment")
    return jax.shard_map(
        on_device, mesh=mesh, in_specs=in_specs, out_specs=out_specs, check_vma=False
    )
```

profile of v0, /device:TPU:12, one launch (start us, length us, event | category | flops | bytes accessed | tf_op | source)
XLA Modules:
  0.0 422.6 jit_solution(14281037983660344813)
XLA Ops:
  0.0 2.7 select_select_fusion
  2.7 6.3 %all-to-all-start = ((bf16[4,128,8,256]{3,1,0,2:T(8,128)(2,1)}), bf16[4,128,8,256]{3,1,0,2:T(8,128)(2,1)S(1)}, u32[]{:S(2)}, u32[]{:S(2)}) async-start(bf16[4,128,8,256]{3,1,0,2:T(8,128)(2,1)} %select_select_fusion), calls=%async_computation | async-start | bytes 4194304 | tf_op jit(solution)/shard_map/all_to_all | solution.py:72
  8.9 45.8 %all-to-all-done = bf16[4,128,8,256]{3,1,0,2:T(8,128)(2,1)S(1)} async-done(((bf16[4,128,8,256]{3,1,0,2:T(8,128)(2,1)}), bf16[4,128,8,256]{3,1,0,2:T(8,128)(2,1)S(1)}, u32[]{:S(2)}, u32[]{:S(2)}) %all-to-all-start) | async-done | bytes 2097184 | tf_op jit(solution)/shard_map/all_to_all | solution.py:72
  54.7 2.4 copy.25
  57.1 1.6 broadcast_in_dim.85
  58.7 329.9 %while.18 = (s32[]{:T(128)}, bf16[128,2048]{1,0:T(8,128)(2,1)S(1)}, bf16[4,128,2048]{2,1,0:T(8,128)(2,1)}, pred[]{:T(512)}, pred[]{:T(512)}, /*index=5*/s32[]{:T...) while((s32[]{:T(128)}, bf16[128,2048]{1,0:T(8,128)(2,1)S(1)}, ...), condition=%wide.region_7.8_spmd.clone, body=%wide.region_0.7_spmd.clone.sunk | while | flops 2257898240 | bytes 44399368 | solution.py:140
  58.7 1.1 constant_dynamic-slice_fusion.9
  62.1 23.4 %collective-permute-done = f32[128,2048]{1,0:T(8,128)S(1)} collective-permute-done((f32[128,2048]{1,0:T(8,128)S(1)}, f32[128,2048]{1,0:T(8,128)S(1)}, u32[]{:S(2)}, u32[]{:S(2)}) %collective-permute-start) | collective-permute-done | bytes 1048608 | tf_op jit(solution)/shard_map/while/body/eval_jaxpr/ppermute | solution.py:14
  85.4 1.1 bitcast_dynamic-update-slice_fusion.2
  87.0 1.9 collective-permute-start.1
  88.9 25.8 %collective-permute-done.1 = bf16[128,2048]{1,0:T(8,128)(2,1)S(1)} collective-permute-done((bf16[128,2048]{1,0:T(8,128)(2,1)S(1)}, bf16[128,2048]{1,0:T(8,128)(2,1)S(1)}, u32[]{:S(2)}, u32[]{:S(2)}) %collective-permute-start.1) | collective-permute-done | bytes 524320 | tf_op jit(solution)/shard_map/while/body/eval_jaxpr/ppermute | solution.py:20
  114.7 1.1 constant_dynamic-slice_fusion.9
  116.1 15.2 %conditional.3 = (f32[128,2048]{1,0:T(8,128)S(1)}) conditional(s32[]{:T(128)} %convert_element_type.120, () %tuple.56, (s32[]{:T(128)}, bf16[128,2048]{1,0:T(8,128)(2,1)S(1)}, f32[2048]{0:T(1024)S(1)}, bf16[128,2048]{1,0:T(8,128)(2,1)S(1)}, bf16[2048,3072]{1,0:T(8,128)(2,1)}, /*index=5*/s32[]{:T(128)}, s32[4]{0:T(128)S(1)}, s32[4]{0:T(128)S(1)}, ...), branch_computations={%region_1.1_spmd, %region_2.5_spmd} | conditional | flops 2254227968 | bytes 27479392 | solution.py:119
  118.9 4.7 %fusion.9 = bf16[128,2048]{1,0:T(8,128)(2,1)S(1)} fusion(bf16[2048,3072]{1,0:T(8,128)(2,1)} %get-tuple-element.369, bf16[128,2048]{1,0:T(8,128)(2,1)S(1)} %get-tuple-element.366, pred[]{:T(512)S(6)} %eq.42, bf16[128,2048]{1,0:T(8,128)(2,1)S(1)} %get-tuple-element.367, f32[2048]{0:T(1024)S(1)} %get-tuple-element.368, f32[128]{0:T(128)S(1)} %add_rsqrt_fusion), kind=kOutput, calls=%fused_computation.7 | convolution fusion | flops 1075314688 | bytes 9970177 | tf_op jit(solution)/shard_map/while/body/eval_jaxpr/cond/branch_1_fun/dot_general | solution.py:95
  123.9 2.9 fusion.15
  128.4 2.9 fusion.35
  131.4 2.1 collective-permute-start
  134.5 19.9 %collective-permute-done = f32[128,2048]{1,0:T(8,128)S(1)} collective-permute-done((f32[128,2048]{1,0:T(8,128)S(1)}, f32[128,2048]{1,0:T(8,128)S(1)}, u32[]{:S(2)}, u32[]{:S(2)}) %collective-permute-start) | collective-permute-done | bytes 1048608 | tf_op jit(solution)/shard_map/while/body/eval_jaxpr/ppermute | solution.py:14
  154.5 1.1 bitcast_dynamic-update-slice_fusion.2
  156.0 1.9 collective-permute-start.1
  158.0 10.9 %collective-permute-done.1 = bf16[128,2048]{1,0:T(8,128)(2,1)S(1)} collective-permute-done((bf16[128,2048]{1,0:T(8,128)(2,1)S(1)}, bf16[128,2048]{1,0:T(8,128)(2,1)S(1)}, u32[]{:S(2)}, u32[]{:S(2)}) %collective-permute-start.1) | collective-permute-done | bytes 524320 | tf_op jit(solution)/shard_map/while/body/eval_jaxpr/ppermute | solution.py:20
  168.8 1.1 constant_dynamic-slice_fusion.9
  170.3 15.2 %conditional.3 = (f32[128,2048]{1,0:T(8,128)S(1)}) conditional(s32[]{:T(128)} %convert_element_type.120, () %tuple.56, (s32[]{:T(128)}, bf16[128,2048]{1,0:T(8,128)(2,1)S(1)}, f32[2048]{0:T(1024)S(1)}, bf16[128,2048]{1,0:T(8,128)(2,1)S(1)}, bf16[2048,3072]{1,0:T(8,128)(2,1)}, /*index=5*/s32[]{:T(128)}, s32[4]{0:T(128)S(1)}, s32[4]{0:T(128)S(1)}, ...), branch_computations={%region_1.1_spmd, %region_2.5_spmd} | conditional | flops 2254227968 | bytes 27479392 | solution.py:119
  173.0 4.7 %fusion.9 = bf16[128,2048]{1,0:T(8,128)(2,1)S(1)} fusion(bf16[2048,3072]{1,0:T(8,128)(2,1)} %get-tuple-element.369, bf16[128,2048]{1,0:T(8,128)(2,1)S(1)} %get-tuple-element.366, pred[]{:T(512)S(6)} %eq.42, bf16[128,2048]{1,0:T(8,128)(2,1)S(1)} %get-tuple-element.367, f32[2048]{0:T(1024)S(1)} %get-tuple-element.368, f32[128]{0:T(128)S(1)} %add_rsqrt_fusion), kind=kOutput, calls=%fused_computation.7 | convolution fusion | flops 1075314688 | bytes 9970177 | tf_op jit(solution)/shard_map/while/body/eval_jaxpr/cond/branch_1_fun/dot_general | solution.py:95
  178.0 3.0 fusion.15
  182.6 2.9 fusion.35
  185.5 1.5 collective-permute-start
  188.1 18.7 %collective-permute-done = f32[128,2048]{1,0:T(8,128)S(1)} collective-permute-done((f32[128,2048]{1,0:T(8,128)S(1)}, f32[128,2048]{1,0:T(8,128)S(1)}, u32[]{:S(2)}, u32[]{:S(2)}) %collective-permute-start) | collective-permute-done | bytes 1048608 | tf_op jit(solution)/shard_map/while/body/eval_jaxpr/ppermute | solution.py:14
  206.9 1.1 bitcast_dynamic-update-slice_fusion.2
  208.4 2.5 collective-permute-start.1
  210.9 8.6 %collective-permute-done.1 = bf16[128,2048]{1,0:T(8,128)(2,1)S(1)} collective-permute-done((bf16[128,2048]{1,0:T(8,128)(2,1)S(1)}, bf16[128,2048]{1,0:T(8,128)(2,1)S(1)}, u32[]{:S(2)}, u32[]{:S(2)}) %collective-permute-start.1) | collective-permute-done | bytes 524320 | tf_op jit(solution)/shard_map/while/body/eval_jaxpr/ppermute | solution.py:20
  219.5 1.1 constant_dynamic-slice_fusion.9
  221.0 15.2 %conditional.3 = (f32[128,2048]{1,0:T(8,128)S(1)}) conditional(s32[]{:T(128)} %convert_element_type.120, () %tuple.56, (s32[]{:T(128)}, bf16[128,2048]{1,0:T(8,128)(2,1)S(1)}, f32[2048]{0:T(1024)S(1)}, bf16[128,2048]{1,0:T(8,128)(2,1)S(1)}, bf16[2048,3072]{1,0:T(8,128)(2,1)}, /*index=5*/s32[]{:T(128)}, s32[4]{0:T(128)S(1)}, s32[4]{0:T(128)S(1)}, ...), branch_computations={%region_1.1_spmd, %region_2.5_spmd} | conditional | flops 2254227968 | bytes 27479392 | solution.py:119
  223.7 4.7 %fusion.9 = bf16[128,2048]{1,0:T(8,128)(2,1)S(1)} fusion(bf16[2048,3072]{1,0:T(8,128)(2,1)} %get-tuple-element.369, bf16[128,2048]{1,0:T(8,128)(2,1)S(1)} %get-tuple-element.366, pred[]{:T(512)S(6)} %eq.42, bf16[128,2048]{1,0:T(8,128)(2,1)S(1)} %get-tuple-element.367, f32[2048]{0:T(1024)S(1)} %get-tuple-element.368, f32[128]{0:T(128)S(1)} %add_rsqrt_fusion), kind=kOutput, calls=%fused_computation.7 | convolution fusion | flops 1075314688 | bytes 9970177 | tf_op jit(solution)/shard_map/while/body/eval_jaxpr/cond/branch_1_fun/dot_general | solution.py:95
  228.7 3.0 fusion.15
  233.2 2.9 fusion.35
  236.2 1.2 collective-permute-start
  238.5 17.3 %collective-permute-done = f32[128,2048]{1,0:T(8,128)S(1)} collective-permute-done((f32[128,2048]{1,0:T(8,128)S(1)}, f32[128,2048]{1,0:T(8,128)S(1)}, u32[]{:S(2)}, u32[]{:S(2)}) %collective-permute-start) | collective-permute-done | bytes 1048608 | tf_op jit(solution)/shard_map/while/body/eval_jaxpr/ppermute | solution.py:14
  255.8 1.1 bitcast_dynamic-update-slice_fusion.2
  257.4 3.1 collective-permute-start.1
  260.5 8.0 %collective-permute-done.1 = bf16[128,2048]{1,0:T(8,128)(2,1)S(1)} collective-permute-done((bf16[128,2048]{1,0:T(8,128)(2,1)S(1)}, bf16[128,2048]{1,0:T(8,128)(2,1)S(1)}, u32[]{:S(2)}, u32[]{:S(2)}) %collective-permute-start.1) | collective-permute-done | bytes 524320 | tf_op jit(solution)/shard_map/while/body/eval_jaxpr/ppermute | solution.py:20
  268.5 1.1 constant_dynamic-slice_fusion.9
  269.9 15.2 %conditional.3 = (f32[128,2048]{1,0:T(8,128)S(1)}) conditional(s32[]{:T(128)} %convert_element_type.120, () %tuple.56, (s32[]{:T(128)}, bf16[128,2048]{1,0:T(8,128)(2,1)S(1)}, f32[2048]{0:T(1024)S(1)}, bf16[128,2048]{1,0:T(8,128)(2,1)S(1)}, bf16[2048,3072]{1,0:T(8,128)(2,1)}, /*index=5*/s32[]{:T(128)}, s32[4]{0:T(128)S(1)}, s32[4]{0:T(128)S(1)}, ...), branch_computations={%region_1.1_spmd, %region_2.5_spmd} | conditional | flops 2254227968 | bytes 27479392 | solution.py:119
  272.7 4.7 %fusion.9 = bf16[128,2048]{1,0:T(8,128)(2,1)S(1)} fusion(bf16[2048,3072]{1,0:T(8,128)(2,1)} %get-tuple-element.369, bf16[128,2048]{1,0:T(8,128)(2,1)S(1)} %get-tuple-element.366, pred[]{:T(512)S(6)} %eq.42, bf16[128,2048]{1,0:T(8,128)(2,1)S(1)} %get-tuple-element.367, f32[2048]{0:T(1024)S(1)} %get-tuple-element.368, f32[128]{0:T(128)S(1)} %add_rsqrt_fusion), kind=kOutput, calls=%fused_computation.7 | convolution fusion | flops 1075314688 | bytes 9970177 | tf_op jit(solution)/shard_map/while/body/eval_jaxpr/cond/branch_1_fun/dot_general | solution.py:95
  277.6 2.9 fusion.15
  282.2 2.9 fusion.35
  286.9 15.9 %collective-permute-done = f32[128,2048]{1,0:T(8,128)S(1)} collective-permute-done((f32[128,2048]{1,0:T(8,128)S(1)}, f32[128,2048]{1,0:T(8,128)S(1)}, u32[]{:S(2)}, u32[]{:S(2)}) %collective-permute-start) | collective-permute-done | bytes 1048608 | tf_op jit(solution)/shard_map/while/body/eval_jaxpr/ppermute | solution.py:14
  302.7 1.1 bitcast_dynamic-update-slice_fusion.2
  304.3 3.4 collective-permute-start.1
  307.7 7.7 %collective-permute-done.1 = bf16[128,2048]{1,0:T(8,128)(2,1)S(1)} collective-permute-done((bf16[128,2048]{1,0:T(8,128)(2,1)S(1)}, bf16[128,2048]{1,0:T(8,128)(2,1)S(1)}, u32[]{:S(2)}, u32[]{:S(2)}) %collective-permute-start.1) | collective-permute-done | bytes 524320 | tf_op jit(solution)/shard_map/while/body/eval_jaxpr/ppermute | solution.py:20
  318.4 14.2 %collective-permute-done = f32[128,2048]{1,0:T(8,128)S(1)} collective-permute-done((f32[128,2048]{1,0:T(8,128)S(1)}, f32[128,2048]{1,0:T(8,128)S(1)}, u32[]{:S(2)}, u32[]{:S(2)}) %collective-permute-start) | collective-permute-done | bytes 1048608 | tf_op jit(solution)/shard_map/while/body/eval_jaxpr/ppermute | solution.py:14
  332.6 1.1 bitcast_dynamic-update-slice_fusion.2
  334.1 18.8 %collective-permute-start.1 = (bf16[128,2048]{1,0:T(8,128)(2,1)S(1)}, bf16[128,2048]{1,0:T(8,128)(2,1)S(1)}, u32[]{:S(2)}, u32[]{:S(2)}) collective-permute-start(bf16[128,2048]{1,0:T(8,128)(2,1)S(1)} %fusion.47), channel_id=1, source_target_pairs={{0,8},{4,12},{8,16},{12,20},{16,24},{20,28},{1,9},{5,13},{9,17},{1... | collective-permute-start | bytes 1572872 | tf_op jit(solution)/shard_map/while/body/eval_jaxpr/ppermute | solution.py:20
  352.9 6.7 %collective-permute-done.1 = bf16[128,2048]{1,0:T(8,128)(2,1)S(1)} collective-permute-done((bf16[128,2048]{1,0:T(8,128)(2,1)S(1)}, bf16[128,2048]{1,0:T(8,128)(2,1)S(1)}, u32[]{:S(2)}, u32[]{:S(2)}) %collective-permute-start.1) | collective-permute-done | bytes 524320 | tf_op jit(solution)/shard_map/while/body/eval_jaxpr/ppermute | solution.py:20
  362.5 13.4 %collective-permute-done = f32[128,2048]{1,0:T(8,128)S(1)} collective-permute-done((f32[128,2048]{1,0:T(8,128)S(1)}, f32[128,2048]{1,0:T(8,128)S(1)}, u32[]{:S(2)}, u32[]{:S(2)}) %collective-permute-start) | collective-permute-done | bytes 1048608 | tf_op jit(solution)/shard_map/while/body/eval_jaxpr/ppermute | solution.py:14
  376.0 1.1 bitcast_dynamic-update-slice_fusion.2
  377.5 4.4 %collective-permute-start.1 = (bf16[128,2048]{1,0:T(8,128)(2,1)S(1)}, bf16[128,2048]{1,0:T(8,128)(2,1)S(1)}, u32[]{:S(2)}, u32[]{:S(2)}) collective-permute-start(bf16[128,2048]{1,0:T(8,128)(2,1)S(1)} %fusion.47), channel_id=1, source_target_pairs={{0,8},{4,12},{8,16},{12,20},{16,24},{20,28},{1,9},{5,13},{9,17},{1... | collective-permute-start | bytes 1572872 | tf_op jit(solution)/shard_map/while/body/eval_jaxpr/ppermute | solution.py:20
  381.9 6.7 %collective-permute-done.1 = bf16[128,2048]{1,0:T(8,128)(2,1)S(1)} collective-permute-done((bf16[128,2048]{1,0:T(8,128)(2,1)S(1)}, bf16[128,2048]{1,0:T(8,128)(2,1)S(1)}, u32[]{:S(2)}, u32[]{:S(2)}) %collective-permute-start.1) | collective-permute-done | bytes 524320 | tf_op jit(solution)/shard_map/while/body/eval_jaxpr/ppermute | solution.py:20
  388.6 1.2 constant_dynamic-slice_fusion.2
  390.5 1.3 collective-permute-start.3
  391.8 2.1 collective-permute-start.4
  393.9 22.6 %collective-permute-done.3 = bf16[4,128,256]{2,1,0:T(8,128)(2,1)S(1)} collective-permute-done((bf16[4,128,256]{2,1,0:T(8,128)(2,1)S(1)}, bf16[4,128,256]{2,1,0:T(8,128)(2,1)S(1)}, u32[]{:S(2)}, u32[]{:S(2)}) %collective-permute-start.3) | collective-permute-done | bytes 262176 | tf_op jit(solution)/shard_map/ppermute | solution.py:20
  416.5 4.3 %collective-permute-done.4 = bf16[4,128,256]{2,1,0:T(8,128)(2,1)S(1)} collective-permute-done((bf16[4,128,256]{2,1,0:T(8,128)(2,1)S(1)}, bf16[4,128,256]{2,1,0:T(8,128)(2,1)S(1)}, u32[]{:S(2)}, u32[]{:S(2)}) %collective-permute-start.4) | collective-permute-done | bytes 262176 | tf_op jit(solution)/shard_map/ppermute | solution.py:20
  420.8 1.8 select_select_fusion.1
  (140 shorter events, 31.6 us)
Async XLA Ops:
  0.0 8.9 %copy-start = (f32[4,2048]{1,0:T(4,128)S(1)}, f32[4,2048]{1,0:T(4,128)}, u32[]{:S(2)}) copy-start(f32[4,2048]{1,0:T(4,128)} %param.18) | copy-start | bytes 98308
  2.7 52.0 %all-to-all-start = ((bf16[4,128,8,256]{3,1,0,2:T(8,128)(2,1)}), bf16[4,128,8,256]{3,1,0,2:T(8,128)(2,1)S(1)}, u32[]{:S(2)}, u32[]{:S(2)}) async-start(bf16[4,128,8,256]{3,1,0,2:T(8,128)(2,1)} %select_select_fusion), calls=%async_computation | async-start | bytes 4194304 | tf_op jit(solution)/shard_map/all_to_all | solution.py:72
  57.1 1.6 copy-start.1
  57.1 1.6 copy-start.2
  57.1 1.6 copy-start.3
  60.3 25.1 %collective-permute-start = (f32[128,2048]{1,0:T(8,128)S(1)}, f32[128,2048]{1,0:T(8,128)S(1)}, u32[]{:S(2)}, u32[]{:S(2)}) collective-permute-start(f32[128,2048]{1,0:T(8,128)S(1)} %get-tuple-element.623), channel_id=1, source_target_pairs={{0,4},{4,0},{8,12},{12,8},{16,20},{20,16},{24,28},{28,24},{1,5},{5... | collective-permute-start | bytes 3145736 | tf_op jit(solution)/shard_map/while/body/eval_jaxpr/ppermute | solution.py:14
  87.0 27.7 %collective-permute-start.1 = (bf16[128,2048]{1,0:T(8,128)(2,1)S(1)}, bf16[128,2048]{1,0:T(8,128)(2,1)S(1)}, u32[]{:S(2)}, u32[]{:S(2)}) collective-permute-start(bf16[128,2048]{1,0:T(8,128)(2,1)S(1)} %fusion.47), channel_id=1, source_target_pairs={{0,8},{4,12},{8,16},{12,20},{16,24},{20,28},{1,9},{5,13},{9,17},{1... | collective-permute-start | bytes 1572872 | tf_op jit(solution)/shard_map/while/body/eval_jaxpr/ppermute | solution.py:20
  131.4 23.1 %collective-permute-start = (f32[128,2048]{1,0:T(8,128)S(1)}, f32[128,2048]{1,0:T(8,128)S(1)}, u32[]{:S(2)}, u32[]{:S(2)}) collective-permute-start(f32[128,2048]{1,0:T(8,128)S(1)} %get-tuple-element.623), channel_id=1, source_target_pairs={{0,4},{4,0},{8,12},{12,8},{16,20},{20,16},{24,28},{28,24},{1,5},{5... | collective-permute-start | bytes 3145736 | tf_op jit(solution)/shard_map/while/body/eval_jaxpr/ppermute | solution.py:14
  156.0 12.8 %collective-permute-start.1 = (bf16[128,2048]{1,0:T(8,128)(2,1)S(1)}, bf16[128,2048]{1,0:T(8,128)(2,1)S(1)}, u32[]{:S(2)}, u32[]{:S(2)}) collective-permute-start(bf16[128,2048]{1,0:T(8,128)(2,1)S(1)} %fusion.47), channel_id=1, source_target_pairs={{0,8},{4,12},{8,16},{12,20},{16,24},{20,28},{1,9},{5,13},{9,17},{1... | collective-permute-start | bytes 1572872 | tf_op jit(solution)/shard_map/while/body/eval_jaxpr/ppermute | solution.py:20
  185.5 21.4 %collective-permute-start = (f32[128,2048]{1,0:T(8,128)S(1)}, f32[128,2048]{1,0:T(8,128)S(1)}, u32[]{:S(2)}, u32[]{:S(2)}) collective-permute-start(f32[128,2048]{1,0:T(8,128)S(1)} %get-tuple-element.623), channel_id=1, source_target_pairs={{0,4},{4,0},{8,12},{12,8},{16,20},{20,16},{24,28},{28,24},{1,5},{5... | collective-permute-start | bytes 3145736 | tf_op jit(solution)/shard_map/while/body/eval_jaxpr/ppermute | solution.py:14
  208.4 11.1 %collective-permute-start.1 = (bf16[128,2048]{1,0:T(8,128)(2,1)S(1)}, bf16[128,2048]{1,0:T(8,128)(2,1)S(1)}, u32[]{:S(2)}, u32[]{:S(2)}) collective-permute-start(bf16[128,2048]{1,0:T(8,128)(2,1)S(1)} %fusion.47), channel_id=1, source_target_pairs={{0,8},{4,12},{8,16},{12,20},{16,24},{20,28},{1,9},{5,13},{9,17},{1... | collective-permute-start | bytes 1572872 | tf_op jit(solution)/shard_map/while/body/eval_jaxpr/ppermute | solution.py:20
  236.2 19.6 %collective-permute-start = (f32[128,2048]{1,0:T(8,128)S(1)}, f32[128,2048]{1,0:T(8,128)S(1)}, u32[]{:S(2)}, u32[]{:S(2)}) collective-permute-start(f32[128,2048]{1,0:T(8,128)S(1)} %get-tuple-element.623), channel_id=1, source_target_pairs={{0,4},{4,0},{8,12},{12,8},{16,20},{20,16},{24,28},{28,24},{1,5},{5... | collective-permute-start | bytes 3145736 | tf_op jit(solution)/shard_map/while/body/eval_jaxpr/ppermute | solution.py:14
  257.4 11.1 %collective-permute-start.1 = (bf16[128,2048]{1,0:T(8,128)(2,1)S(1)}, bf16[128,2048]{1,0:T(8,128)(2,1)S(1)}, u32[]{:S(2)}, u32[]{:S(2)}) collective-permute-start(bf16[128,2048]{1,0:T(8,128)(2,1)S(1)} %fusion.47), channel_id=1, source_target_pairs={{0,8},{4,12},{8,16},{12,20},{16,24},{20,28},{1,9},{5,13},{9,17},{1... | collective-permute-start | bytes 1572872 | tf_op jit(solution)/shard_map/while/body/eval_jaxpr/ppermute | solution.py:20
  285.1 17.6 %collective-permute-start = (f32[128,2048]{1,0:T(8,128)S(1)}, f32[128,2048]{1,0:T(8,128)S(1)}, u32[]{:S(2)}, u32[]{:S(2)}) collective-permute-start(f32[128,2048]{1,0:T(8,128)S(1)} %get-tuple-element.623), channel_id=1, source_target_pairs={{0,4},{4,0},{8,12},{12,8},{16,20},{20,16},{24,28},{28,24},{1,5},{5... | collective-permute-start | bytes 3145736 | tf_op jit(solution)/shard_map/while/body/eval_jaxpr/ppermute | solution.py:14
  304.3 11.1 %collective-permute-start.1 = (bf16[128,2048]{1,0:T(8,128)(2,1)S(1)}, bf16[128,2048]{1,0:T(8,128)(2,1)S(1)}, u32[]{:S(2)}, u32[]{:S(2)}) collective-permute-start(bf16[128,2048]{1,0:T(8,128)(2,1)S(1)} %fusion.47), channel_id=1, source_target_pairs={{0,8},{4,12},{8,16},{12,20},{16,24},{20,28},{1,9},{5,13},{9,17},{1... | collective-permute-start | bytes 1572872 | tf_op jit(solution)/shard_map/while/body/eval_jaxpr/ppermute | solution.py:20
  316.9 15.6 %collective-permute-start = (f32[128,2048]{1,0:T(8,128)S(1)}, f32[128,2048]{1,0:T(8,128)S(1)}, u32[]{:S(2)}, u32[]{:S(2)}) collective-permute-start(f32[128,2048]{1,0:T(8,128)S(1)} %get-tuple-element.623), channel_id=1, source_target_pairs={{0,4},{4,0},{8,12},{12,8},{16,20},{20,16},{24,28},{28,24},{1,5},{5... | collective-permute-start | bytes 3145736 | tf_op jit(solution)/shard_map/while/body/eval_jaxpr/ppermute | solution.py:14
  334.1 25.5 %collective-permute-start.1 = (bf16[128,2048]{1,0:T(8,128)(2,1)S(1)}, bf16[128,2048]{1,0:T(8,128)(2,1)S(1)}, u32[]{:S(2)}, u32[]{:S(2)}) collective-permute-start(bf16[128,2048]{1,0:T(8,128)(2,1)S(1)} %fusion.47), channel_id=1, source_target_pairs={{0,8},{4,12},{8,16},{12,20},{16,24},{20,28},{1,9},{5,13},{9,17},{1... | collective-permute-start | bytes 1572872 | tf_op jit(solution)/shard_map/while/body/eval_jaxpr/ppermute | solution.py:20
  361.1 14.9 %collective-permute-start = (f32[128,2048]{1,0:T(8,128)S(1)}, f32[128,2048]{1,0:T(8,128)S(1)}, u32[]{:S(2)}, u32[]{:S(2)}) collective-permute-start(f32[128,2048]{1,0:T(8,128)S(1)} %get-tuple-element.623), channel_id=1, source_target_pairs={{0,4},{4,0},{8,12},{12,8},{16,20},{20,16},{24,28},{28,24},{1,5},{5... | collective-permute-start | bytes 3145736 | tf_op jit(solution)/shard_map/while/body/eval_jaxpr/ppermute | solution.py:14
  377.5 11.1 %collective-permute-start.1 = (bf16[128,2048]{1,0:T(8,128)(2,1)S(1)}, bf16[128,2048]{1,0:T(8,128)(2,1)S(1)}, u32[]{:S(2)}, u32[]{:S(2)}) collective-permute-start(bf16[128,2048]{1,0:T(8,128)(2,1)S(1)} %fusion.47), channel_id=1, source_target_pairs={{0,8},{4,12},{8,16},{12,20},{16,24},{20,28},{1,9},{5,13},{9,17},{1... | collective-permute-start | bytes 1572872 | tf_op jit(solution)/shard_map/while/body/eval_jaxpr/ppermute | solution.py:20
  389.8 4.1 collective-permute-start.2
  390.5 26.0 %collective-permute-start.3 = (bf16[4,128,256]{2,1,0:T(8,128)(2,1)S(1)}, bf16[4,128,256]{2,1,0:T(8,128)(2,1)S(1)}, u32[]{:S(2)}, u32[]{:S(2)}) collective-permute-start(bf16[4,128,256]{2,1,0:T(8,128)(2,1)S(1)} %get-tuple-element.476), channel_id=1, source_target_pairs={{16,0},{20,4},{24,8},{28,12},{17,1},{21,5},{25,9},{29,13},{18,2},{... | collective-permute-start | bytes 786440 | tf_op jit(solution)/shard_map/ppermute | solution.py:20
  391.8 29.0 %collective-permute-start.4 = (bf16[4,128,256]{2,1,0:T(8,128)(2,1)S(1)}, bf16[4,128,256]{2,1,0:T(8,128)(2,1)S(1)}, u32[]{:S(2)}, u32[]{:S(2)}) collective-permute-start(bf16[4,128,256]{2,1,0:T(8,128)(2,1)S(1)} %get-tuple-element.475), channel_id=1, source_target_pairs={{8,0},{12,4},{16,8},{20,12},{24,16},{28,20},{9,1},{13,5},{17,9},{2... | collective-permute-start | bytes 786440 | tf_op jit(solution)/shard_map/ppermute | solution.py:20
where the time goes:
time: 424 us; the launch traced here: 423 us
  waiting for transfers between devices  270 us (64%)
  starting transfers between devices  53.2 us (13%)
  matrix products  47.3 us (11%)
  local copies, waits for them, and re-layouts  29.2 us (7%)
  other arithmetic  16.9 us (4%)
  loops' own time  6.02 us (1%)
    ppermute x7, waiting for transfers between devices, partner(): return lax.ppermute(value, axis, pairs)  123 us
    ppermute x10, waiting for transfers between devices, shifted(): return lax.ppermute(value, axis, pairs)  101 us
    all_to_all x1, waiting for transfers between devices, on_device(): lax.all_to_all(outgoing, 'segment', split_axis=2, concat_axis=2, tiled=True)  45.8 us
    ppermute x10, starting transfers between devices, shifted(): return lax.ppermute(value, axis, pairs)  40 us
    dynamic_slice x30, local copies, waits for them, and re-layouts, pick_row(): return lax.dynamic_index_in_dim(array, row_slot, 0, keepdims=False)  21.5 us
    dot_general x4, matrix products, head_partial(): jnp.dot(source, in_weight[:, head_cols:], preferred_element_type=jnp.floa...  18.8 us
    dot_general x4, matrix products, head_partial(): jnp.dot(normed, in_weight[:, :head_cols], preferred_element_type=jnp.floa...  11.8 us
    dot_general x4, matrix products, head_partial(): return jnp.dot(mixture, out_weight, preferred_element_type=jnp.float32)  11.7 us
  transfers between devices with their start and end apart: 18, of which 17 were waited for; matrix products, arithmetic and copies ran while one was open for 2% of the time, Pallas kernels for 0%

commit v1 on v0

--- a/solution.py
+++ b/solution.py
@@ -6,6 +6,17 @@
 HEAD = 64
 epsilon = 1e-06
 score_scale = 0.125
+
+
+def cut_along(array, dim, peers):
+    before, after = (array.shape[:dim], array.shape[dim + 1 :])
+    return jnp.moveaxis(array.reshape(*before, peers, -1, *after), dim, 0)
+
+
+def laid_out(blocks, dim):
+    blocks = jnp.moveaxis(blocks, 0, dim)
+    shape = blocks.shape
+    return blocks.reshape(*shape[:dim], shape[dim] * shape[dim + 1], *shape[dim + 2 :])
 
 
 def partner(value, axis, distance):
@@ -69,7 +80,14 @@
         src_embed[:, :, None, :],
         jnp.where(destination == 2, tgt_embed[:, :, None, :], jnp.zeros((), jnp.bfloat16)),
     )
-    arrived = lax.all_to_all(outgoing, "segment", split_axis=2, concat_axis=2, tiled=True)
+    devices, index = (lax.axis_size("segment"), lax.axis_index("segment"))
+    parts = cut_along(outgoing, 2, devices)
+    done = [parts[index]]
+    for step in range(1, devices):
+        sent = parts[index ^ step]
+        done.append(lax.ppermute(sent, "segment", [(i_2, i_2 ^ step) for i_2 in range(devices)]))
+    parts = jnp.stack(done)[index ^ jnp.arange(devices)]
+    arrived = laid_out(parts, 2)
     embedded = arrived.reshape(batches, seq_len, full_width)
     in_weight = attn_in[0]
     out_weight = attn_out[0]

time: 424 us -> 401 us (0.946)
  waiting for transfers between devices: 270 us -> 235 us
  local copies, waits for them, and re-layouts: 29.2 us -> 38.5 us
    all_to_all x1 -> x0, waiting for transfers between devices: 45.8 us -> none  [on_device(): lax.all_to_all(outgoing, 'segment', split_axis=2, concat_axis=2, tiled=True)]
    ppermute x0 -> x7, waiting for transfers between devices: none -> 36.9 us  [on_device(): lax.ppermute(sent, 'segment', [(i_2, i_2 ^ step) for i_2 in range(devices)])]
    ppermute x10, waiting for transfers between devices: 101 us -> 82.2 us  [shifted(): return lax.ppermute(value, axis, pairs)]
    ppermute x0 -> x7, starting transfers between devices: none -> 9.08 us  [on_device(): lax.ppermute(sent, 'segment', [(i_2, i_2 ^ step) for i_2 in range(devices)])]
    ppermute x7, waiting for transfers between devices: 123 us -> 116 us  [partner(): return lax.ppermute(value, axis, pairs)]
    all_to_all x1 -> x0, starting transfers between devices: 6.25 us -> none  [on_device(): lax.all_to_all(outgoing, 'segment', split_axis=2, concat_axis=2, tiled=True)]
    unnamed x8 -> x15, local copies, waits for them, and re-layouts: 0.02 us -> 5.04 us
  transfers between devices with their start and end apart: 18 -> 24, of which waited for: 17 -> 22; matrix products, arithmetic and copies ran while one was open for 2% -> 3% of each run, Pallas kernels for 0% -> 0%
where the time goes in v1:
time: 401 us; the launch traced here: 398 us
  waiting for transfers between devices  235 us (59%)
  starting transfers between devices  55 us (14%)
  matrix products  47.3 us (12%)
  local copies, waits for them, and re-layouts  38.5 us (10%)
  other arithmetic  15.6 us (4%)
  loops' own time  6.15 us (2%)
    ppermute x7, waiting for transfers between devices, partner(): return lax.ppermute(value, axis, pairs)  116 us
    ppermute x10, waiting for transfers between devices, shifted(): return lax.ppermute(value, axis, pairs)  82.2 us
    ppermute x10, starting transfers between devices, shifted(): return lax.ppermute(value, axis, pairs)  41.4 us
    ppermute x7, waiting for transfers between devices, on_device(): lax.ppermute(sent, 'segment', [(i_2, i_2 ^ step) for i_2 in range(devices)])  36.9 us
    dynamic_slice x30, local copies, waits for them, and re-layouts, pick_row(): return lax.dynamic_index_in_dim(array, row_slot, 0, keepdims=False)  21.6 us
    dot_general x4, matrix products, head_partial(): jnp.dot(source, in_weight[:, head_cols:], preferred_element_type=jnp.floa...  18.8 us
    dot_general x4, matrix products, head_partial(): jnp.dot(normed, in_weight[:, :head_cols], preferred_element_type=jnp.floa...  11.8 us
    dot_general x4, matrix products, head_partial(): return jnp.dot(mixture, out_weight, preferred_element_type=jnp.float32)  11.7 us
  transfers between devices with their start and end apart: 24, of which 22 were waited for; matrix products, arithmetic and copies ran while one was open for 3% of the time, Pallas kernels for 0%

profile of v1, /device:TPU:12, one launch (start us, length us, event | category | flops | bytes accessed | tf_op | source)
XLA Modules:
  0.0 398.0 jit_solution(405029556286311442)
XLA Ops:
  0.1 1.3 select_select_fusion
  1.4 1.2 dynamic-slice_bitcast_fusion
  2.5 1.5 collective-permute-start.2
  4.5 1.5 collective-permute-start.4
  6.0 2.6 collective-permute-start.5
  9.4 1.3 collective-permute-start.6
  11.8 1.6 collective-permute-start.7
  13.3 8.4 %collective-permute-done.3 = bf16[4,128,1,256]{3,1,0,2:T(8,128)(2,1)S(1)} collective-permute-done((bf16[4,128,1,256]{3,1,0,2:T(8,128)(2,1)}, bf16[4,128,1,256]{3,1,0,2:T(8,128)(2,1)S(1)}, u32[]{:S(2)}, u32[]{:S(2)}) %collective-permute-start.3) | collective-permute-done | bytes 262176 | tf_op jit(solution)/shard_map/ppermute | solution.py:88
  22.7 3.3 collective-permute-done.4
  27.4 16.3 %collective-permute-done.6 = bf16[4,128,1,256]{3,1,0,2:T(8,128)(2,1)S(1)} collective-permute-done((bf16[4,128,1,256]{3,1,0,2:T(8,128)(2,1)}, bf16[4,128,1,256]{3,1,0,2:T(8,128)(2,1)S(1)}, u32[]{:S(2)}, u32[]{:S(2)}) %collective-permute-start.6) | collective-permute-done | bytes 262176 | tf_op jit(solution)/shard_map/ppermute | solution.py:88
  44.4 4.9 %collective-permute-done.7 = bf16[4,128,1,256]{3,1,0,2:T(8,128)(2,1)S(1)} collective-permute-done((bf16[4,128,1,256]{3,1,0,2:T(8,128)(2,1)}, bf16[4,128,1,256]{3,1,0,2:T(8,128)(2,1)S(1)}, u32[]{:S(2)}, u32[]{:S(2)}) %collective-permute-start.7) | collective-permute-done | bytes 262176 | tf_op jit(solution)/shard_map/ppermute | solution.py:88
  50.1 3.6 collective-permute-done.8
  54.4 2.3 gather_fusion
  56.6 2.4 copy.23
  59.0 1.6 broadcast_in_dim.86
  60.7 304.5 %while.18 = (s32[]{:T(128)}, bf16[128,2048]{1,0:T(8,128)(2,1)S(1)}, bf16[4,128,2048]{2,1,0:T(8,128)(2,1)}, pred[]{:T(512)}, pred[]{:T(512)}, /*index=5*/s32[]{:T...) while((s32[]{:T(128)}, bf16[128,2048]{1,0:T(8,128)(2,1)S(1)}, ...), condition=%wide.region_7.8_spmd.clone, body=%wide.region_0.7_spmd.clone.sunk | while | flops 2257898240 | bytes 44399368 | solution.py:158
  64.2 21.4 %collective-permute-done = f32[128,2048]{1,0:T(8,128)S(1)} collective-permute-done((f32[128,2048]{1,0:T(8,128)S(1)}, f32[128,2048]{1,0:T(8,128)S(1)}, u32[]{:S(2)}, u32[]{:S(2)}) %collective-permute-start) | collective-permute-done | bytes 1048608 | tf_op jit(solution)/shard_map/while/body/eval_jaxpr/ppermute | solution.py:25
  85.6 1.1 bitcast_dynamic-update-slice_fusion.10
  87.1 4.6 %collective-permute-start.1 = (bf16[128,2048]{1,0:T(8,128)(2,1)S(1)}, bf16[128,2048]{1,0:T(8,128)(2,1)S(1)}, u32[]{:S(2)}, u32[]{:S(2)}) collective-permute-start(bf16[128,2048]{1,0:T(8,128)(2,1)S(1)} %fusion.48), channel_id=1, source_target_pairs={{0,8},{4,12},{8,16},{12,20},{16,24},{20,28},{1,9},{5,13},{9,17},{1... | collective-permute-start | bytes 1572872 | tf_op jit(solution)/shard_map/while/body/eval_jaxpr/ppermute | solution.py:31
  91.8 8.7 %collective-permute-done.1 = bf16[128,2048]{1,0:T(8,128)(2,1)S(1)} collective-permute-done((bf16[128,2048]{1,0:T(8,128)(2,1)S(1)}, bf16[128,2048]{1,0:T(8,128)(2,1)S(1)}, u32[]{:S(2)}, u32[]{:S(2)}) %collective-permute-start.1) | collective-permute-done | bytes 524320 | tf_op jit(solution)/shard_map/while/body/eval_jaxpr/ppermute | solution.py:31
  101.8 15.3 %conditional.3 = (f32[128,2048]{1,0:T(8,128)S(1)}) conditional(s32[]{:T(128)} %convert_element_type.120, () %tuple.62, (s32[]{:T(128)}, bf16[128,2048]{1,0:T(8,128)(2,1)S(1)}, f32[2048]{0:T(1024)S(1)}, bf16[128,2048]{1,0:T(8,128)(2,1)S(1)}, bf16[2048,3072]{1,0:T(8,128)(2,1)}, /*index=5*/s32[]{:T(128)}, s32[4]{0:T(128)S(1)}, s32[4]{0:T(128)S(1)}, ...), branch_computations={%region_1.1_spmd, %region_2.5_spmd} | conditional | flops 2254227968 | bytes 27479392 | solution.py:137
  104.7 4.7 %fusion.9 = bf16[128,2048]{1,0:T(8,128)(2,1)S(1)} fusion(bf16[2048,3072]{1,0:T(8,128)(2,1)} %get-tuple-element.369, bf16[128,2048]{1,0:T(8,128)(2,1)S(1)} %get-tuple-element.366, pred[]{:T(512)S(6)} %eq.42, bf16[128,2048]{1,0:T(8,128)(2,1)S(1)} %get-tuple-element.367, f32[2048]{0:T(1024)S(1)} %get-tuple-element.368, f32[128]{0:T(128)S(1)} %add_rsqrt_fusion), kind=kOutput, calls=%fused_computation.8 | convolution fusion | flops 1075314688 | bytes 9970177 | tf_op jit(solution)/shard_map/while/body/eval_jaxpr/cond/branch_1_fun/dot_general | solution.py:113
  109.6 2.9 fusion.15
  114.2 2.9 fusion.36
  117.1 1.4 collective-permute-start
  119.6 19.2 %collective-permute-done = f32[128,2048]{1,0:T(8,128)S(1)} collective-permute-done((f32[128,2048]{1,0:T(8,128)S(1)}, f32[128,2048]{1,0:T(8,128)S(1)}, u32[]{:S(2)}, u32[]{:S(2)}) %collective-permute-start) | collective-permute-done | bytes 1048608 | tf_op jit(solution)/shard_map/while/body/eval_jaxpr/ppermute | solution.py:25
  138.7 1.1 bitcast_dynamic-update-slice_fusion.10
  140.3 1.9 collective-permute-start.1
  142.2 9.4 %collective-permute-done.1 = bf16[128,2048]{1,0:T(8,128)(2,1)S(1)} collective-permute-done((bf16[128,2048]{1,0:T(8,128)(2,1)S(1)}, bf16[128,2048]{1,0:T(8,128)(2,1)S(1)}, u32[]{:S(2)}, u32[]{:S(2)}) %collective-permute-start.1) | collective-permute-done | bytes 524320 | tf_op jit(solution)/shard_map/while/body/eval_jaxpr/ppermute | solution.py:31
  153.1 15.3 %conditional.3 = (f32[128,2048]{1,0:T(8,128)S(1)}) conditional(s32[]{:T(128)} %convert_element_type.120, () %tuple.62, (s32[]{:T(128)}, bf16[128,2048]{1,0:T(8,128)(2,1)S(1)}, f32[2048]{0:T(1024)S(1)}, bf16[128,2048]{1,0:T(8,128)(2,1)S(1)}, bf16[2048,3072]{1,0:T(8,128)(2,1)}, /*index=5*/s32[]{:T(128)}, s32[4]{0:T(128)S(1)}, s32[4]{0:T(128)S(1)}, ...), branch_computations={%region_1.1_spmd, %region_2.5_spmd} | conditional | flops 2254227968 | bytes 27479392 | solution.py:137
  155.9 4.7 %fusion.9 = bf16[128,2048]{1,0:T(8,128)(2,1)S(1)} fusion(bf16[2048,3072]{1,0:T(8,128)(2,1)} %get-tuple-element.369, bf16[128,2048]{1,0:T(8,128)(2,1)S(1)} %get-tuple-element.366, pred[]{:T(512)S(6)} %eq.42, bf16[128,2048]{1,0:T(8,128)(2,1)S(1)} %get-tuple-element.367, f32[2048]{0:T(1024)S(1)} %get-tuple-element.368, f32[128]{0:T(128)S(1)} %add_rsqrt_fusion), kind=kOutput, calls=%fused_computation.8 | convolution fusion | flops 1075314688 | bytes 9970177 | tf_op jit(solution)/shard_map/while/body/eval_jaxpr/cond/branch_1_fun/dot_general | solution.py:113
  160.8 3.0 fusion.15
  165.4 2.9 fusion.36
  169.7 18.5 %collective-permute-done = f32[128,2048]{1,0:T(8,128)S(1)} collective-permute-done((f32[128,2048]{1,0:T(8,128)S(1)}, f32[128,2048]{1,0:T(8,128)S(1)}, u32[]{:S(2)}, u32[]{:S(2)}) %collective-permute-start) | collective-permute-done | bytes 1048608 | tf_op jit(solution)/shard_map/while/body/eval_jaxpr/ppermute | solution.py:25
  188.2 1.1 bitcast_dynamic-update-slice_fusion.10
  189.8 2.5 collective-permute-start.1
  192.3 8.6 %collective-permute-done.1 = bf16[128,2048]{1,0:T(8,128)(2,1)S(1)} collective-permute-done((bf16[128,2048]{1,0:T(8,128)(2,1)S(1)}, bf16[128,2048]{1,0:T(8,128)(2,1)S(1)}, u32[]{:S(2)}, u32[]{:S(2)}) %collective-permute-start.1) | collective-permute-done | bytes 524320 | tf_op jit(solution)/shard_map/while/body/eval_jaxpr/ppermute | solution.py:31
  202.3 15.3 %conditional.3 = (f32[128,2048]{1,0:T(8,128)S(1)}) conditional(s32[]{:T(128)} %convert_element_type.120, () %tuple.62, (s32[]{:T(128)}, bf16[128,2048]{1,0:T(8,128)(2,1)S(1)}, f32[2048]{0:T(1024)S(1)}, bf16[128,2048]{1,0:T(8,128)(2,1)S(1)}, bf16[2048,3072]{1,0:T(8,128)(2,1)}, /*index=5*/s32[]{:T(128)}, s32[4]{0:T(128)S(1)}, s32[4]{0:T(128)S(1)}, ...), branch_computations={%region_1.1_spmd, %region_2.5_spmd} | conditional | flops 2254227968 | bytes 27479392 | solution.py:137
  205.1 4.7 %fusion.9 = bf16[128,2048]{1,0:T(8,128)(2,1)S(1)} fusion(bf16[2048,3072]{1,0:T(8,128)(2,1)} %get-tuple-element.369, bf16[128,2048]{1,0:T(8,128)(2,1)S(1)} %get-tuple-element.366, pred[]{:T(512)S(6)} %eq.42, bf16[128,2048]{1,0:T(8,128)(2,1)S(1)} %get-tuple-element.367, f32[2048]{0:T(1024)S(1)} %get-tuple-element.368, f32[128]{0:T(128)S(1)} %add_rsqrt_fusion), kind=kOutput, calls=%fused_computation.8 | convolution fusion | flops 1075314688 | bytes 9970177 | tf_op jit(solution)/shard_map/while/body/eval_jaxpr/cond/branch_1_fun/dot_general | solution.py:113
  210.1 2.9 fusion.15
  214.6 2.9 fusion.36
  219.0 16.5 %collective-permute-done = f32[128,2048]{1,0:T(8,128)S(1)} collective-permute-done((f32[128,2048]{1,0:T(8,128)S(1)}, f32[128,2048]{1,0:T(8,128)S(1)}, u32[]{:S(2)}, u32[]{:S(2)}) %collective-permute-start) | collective-permute-done | bytes 1048608 | tf_op jit(solution)/shard_map/while/body/eval_jaxpr/ppermute | solution.py:25
  235.5 1.1 bitcast_dynamic-update-slice_fusion.10
  237.0 2.8 collective-permute-start.1
  239.8 8.3 %collective-permute-done.1 = bf16[128,2048]{1,0:T(8,128)(2,1)S(1)} collective-permute-done((bf16[128,2048]{1,0:T(8,128)(2,1)S(1)}, bf16[128,2048]{1,0:T(8,128)(2,1)S(1)}, u32[]{:S(2)}, u32[]{:S(2)}) %collective-permute-start.1) | collective-permute-done | bytes 524320 | tf_op jit(solution)/shard_map/while/body/eval_jaxpr/ppermute | solution.py:31
  249.5 15.3 %conditional.3 = (f32[128,2048]{1,0:T(8,128)S(1)}) conditional(s32[]{:T(128)} %convert_element_type.120, () %tuple.62, (s32[]{:T(128)}, bf16[128,2048]{1,0:T(8,128)(2,1)S(1)}, f32[2048]{0:T(1024)S(1)}, bf16[128,2048]{1,0:T(8,128)(2,1)S(1)}, bf16[2048,3072]{1,0:T(8,128)(2,1)}, /*index=5*/s32[]{:T(128)}, s32[4]{0:T(128)S(1)}, s32[4]{0:T(128)S(1)}, ...), branch_computations={%region_1.1_spmd, %region_2.5_spmd} | conditional | flops 2254227968 | bytes 27479392 | solution.py:137
  252.4 4.7 %fusion.9 = bf16[128,2048]{1,0:T(8,128)(2,1)S(1)} fusion(bf16[2048,3072]{1,0:T(8,128)(2,1)} %get-tuple-element.369, bf16[128,2048]{1,0:T(8,128)(2,1)S(1)} %get-tuple-element.366, pred[]{:T(512)S(6)} %eq.42, bf16[128,2048]{1,0:T(8,128)(2,1)S(1)} %get-tuple-element.367, f32[2048]{0:T(1024)S(1)} %get-tuple-element.368, f32[128]{0:T(128)S(1)} %add_rsqrt_fusion), kind=kOutput, calls=%fused_computation.8 | convolution fusion | flops 1075314688 | bytes 9970177 | tf_op jit(solution)/shard_map/while/body/eval_jaxpr/cond/branch_1_fun/dot_general | solution.py:113
  257.3 3.0 fusion.15
  261.9 2.9 fusion.36
  266.3 14.4 %collective-permute-done = f32[128,2048]{1,0:T(8,128)S(1)} collective-permute-done((f32[128,2048]{1,0:T(8,128)S(1)}, f32[128,2048]{1,0:T(8,128)S(1)}, u32[]{:S(2)}, u32[]{:S(2)}) %collective-permute-start) | collective-permute-done | bytes 1048608 | tf_op jit(solution)/shard_map/while/body/eval_jaxpr/ppermute | solution.py:25
  282.2 3.1 collective-permute-start.1
  285.3 8.0 %collective-permute-done.1 = bf16[128,2048]{1,0:T(8,128)(2,1)S(1)} collective-permute-done((bf16[128,2048]{1,0:T(8,128)(2,1)S(1)}, bf16[128,2048]{1,0:T(8,128)(2,1)S(1)}, u32[]{:S(2)}, u32[]{:S(2)}) %collective-permute-start.1) | collective-permute-done | bytes 524320 | tf_op jit(solution)/shard_map/while/body/eval_jaxpr/ppermute | solution.py:31
  296.3 13.4 %collective-permute-done = f32[128,2048]{1,0:T(8,128)S(1)} collective-permute-done((f32[128,2048]{1,0:T(8,128)S(1)}, f32[128,2048]{1,0:T(8,128)S(1)}, u32[]{:S(2)}, u32[]{:S(2)}) %collective-permute-start) | collective-permute-done | bytes 1048608 | tf_op jit(solution)/shard_map/while/body/eval_jaxpr/ppermute | solution.py:25
  311.3 18.2 %collective-permute-start.1 = (bf16[128,2048]{1,0:T(8,128)(2,1)S(1)}, bf16[128,2048]{1,0:T(8,128)(2,1)S(1)}, u32[]{:S(2)}, u32[]{:S(2)}) collective-permute-start(bf16[128,2048]{1,0:T(8,128)(2,1)S(1)} %fusion.48), channel_id=1, source_target_pairs={{0,8},{4,12},{8,16},{12,20},{16,24},{20,28},{1,9},{5,13},{9,17},{1... | collective-permute-start | bytes 1572872 | tf_op jit(solution)/shard_map/while/body/eval_jaxpr/ppermute | solution.py:31
  329.5 6.7 %collective-permute-done.1 = bf16[128,2048]{1,0:T(8,128)(2,1)S(1)} collective-permute-done((bf16[128,2048]{1,0:T(8,128)(2,1)S(1)}, bf16[128,2048]{1,0:T(8,128)(2,1)S(1)}, u32[]{:S(2)}, u32[]{:S(2)}) %collective-permute-start.1) | collective-permute-done | bytes 524320 | tf_op jit(solution)/shard_map/while/body/eval_jaxpr/ppermute | solution.py:31
  339.7 12.9 %collective-permute-done = f32[128,2048]{1,0:T(8,128)S(1)} collective-permute-done((f32[128,2048]{1,0:T(8,128)S(1)}, f32[128,2048]{1,0:T(8,128)S(1)}, u32[]{:S(2)}, u32[]{:S(2)}) %collective-permute-start) | collective-permute-done | bytes 1048608 | tf_op jit(solution)/shard_map/while/body/eval_jaxpr/ppermute | solution.py:25
  354.1 4.4 %collective-permute-start.1 = (bf16[128,2048]{1,0:T(8,128)(2,1)S(1)}, bf16[128,2048]{1,0:T(8,128)(2,1)S(1)}, u32[]{:S(2)}, u32[]{:S(2)}) collective-permute-start(bf16[128,2048]{1,0:T(8,128)(2,1)S(1)} %fusion.48), channel_id=1, source_target_pairs={{0,8},{4,12},{8,16},{12,20},{16,24},{20,28},{1,9},{5,13},{9,17},{1... | collective-permute-start | bytes 1572872 | tf_op jit(solution)/shard_map/while/body/eval_jaxpr/ppermute | solution.py:31
  358.5 6.7 %collective-permute-done.1 = bf16[128,2048]{1,0:T(8,128)(2,1)S(1)} collective-permute-done((bf16[128,2048]{1,0:T(8,128)(2,1)S(1)}, bf16[128,2048]{1,0:T(8,128)(2,1)S(1)}, u32[]{:S(2)}, u32[]{:S(2)}) %collective-permute-start.1) | collective-permute-done | bytes 524320 | tf_op jit(solution)/shard_map/while/body/eval_jaxpr/ppermute | solution.py:31
  365.2 1.2 constant_dynamic-slice_fusion.2
  366.4 1.3 collective-permute-start.10
  367.7 1.9 collective-permute-start.11
  370.3 19.5 %collective-permute-done.10 = bf16[4,128,256]{2,1,0:T(8,128)(2,1)S(1)} collective-permute-done((bf16[4,128,256]{2,1,0:T(8,128)(2,1)S(1)}, bf16[4,128,256]{2,1,0:T(8,128)(2,1)S(1)}, u32[]{:S(2)}, u32[]{:S(2)}) %collective-permute-start.10) | collective-permute-done | bytes 262176 | tf_op jit(solution)/shard_map/ppermute | solution.py:31
  389.8 6.4 %collective-permute-done.11 = bf16[4,128,256]{2,1,0:T(8,128)(2,1)S(1)} collective-permute-done((bf16[4,128,256]{2,1,0:T(8,128)(2,1)S(1)}, bf16[4,128,256]{2,1,0:T(8,128)(2,1)S(1)}, u32[]{:S(2)}, u32[]{:S(2)}) %collective-permute-start.11) | collective-permute-done | bytes 262176 | tf_op jit(solution)/shard_map/ppermute | solution.py:31
  396.2 1.8 select_select_fusion.1
  (164 shorter events, 48.3 us)
Async XLA Ops:
  0.0 8.6 %copy-start = (f32[4,2048]{1,0:T(4,128)S(1)}, f32[4,2048]{1,0:T(4,128)}, u32[]{:S(2)}) copy-start(f32[4,2048]{1,0:T(4,128)} %param.18) | copy-start | bytes 98308
  2.5 8.5 %collective-permute-start.2 = (bf16[4,128,1,256]{3,1,0,2:T(8,128)(2,1)}, bf16[4,128,1,256]{3,1,0,2:T(8,128)(2,1)S(1)}, u32[]{:S(2)}, u32[]{:S(2)}) collective-permute-start(bf16[4,128,1,256]{3,1,0,2:T(8,128)(2,1)} %get-tuple-element.484), channel_id=1, source_target_pairs={{0,4},{4,0},{8,12},{12,8},{16,20},{20,16},{24,28},{28,24},{1,5},{5... | collective-permute-start | bytes 786440 | tf_op jit(solution)/shard_map/ppermute | solution.py:88
  4.0 17.7 %collective-permute-start.3 = (bf16[4,128,1,256]{3,1,0,2:T(8,128)(2,1)}, bf16[4,128,1,256]{3,1,0,2:T(8,128)(2,1)S(1)}, u32[]{:S(2)}, u32[]{:S(2)}) collective-permute-start(bf16[4,128,1,256]{3,1,0,2:T(8,128)(2,1)} %get-tuple-element.483), channel_id=1, source_target_pairs={{0,8},{4,12},{8,0},{12,4},{16,24},{20,28},{24,16},{28,20},{1,9},{5... | collective-permute-start | bytes 786440 | tf_op jit(solution)/shard_map/ppermute | solution.py:88
  4.5 21.5 %collective-permute-start.4 = (bf16[4,128,1,256]{3,1,0,2:T(8,128)(2,1)}, bf16[4,128,1,256]{3,1,0,2:T(8,128)(2,1)S(1)}, u32[]{:S(2)}, u32[]{:S(2)}) collective-permute-start(bf16[4,128,1,256]{3,1,0,2:T(8,128)(2,1)} %get-tuple-element.482), channel_id=1, source_target_pairs={{0,12},{4,8},{8,4},{12,0},{16,28},{20,24},{24,20},{28,16},{1,13},{... | collective-permute-start | bytes 786440 | tf_op jit(solution)/shard_map/ppermute | solution.py:88
  6.0 20.7 %collective-permute-start.5 = (bf16[4,128,1,256]{3,1,0,2:T(8,128)(2,1)}, bf16[4,128,1,256]{3,1,0,2:T(8,128)(2,1)S(1)}, u32[]{:S(2)}, u32[]{:S(2)}) collective-permute-start(bf16[4,128,1,256]{3,1,0,2:T(8,128)(2,1)} %get-tuple-element.481), channel_id=1, source_target_pairs={{0,16},{4,20},{8,24},{12,28},{16,0},{20,4},{24,8},{28,12},{1,17},{... | collective-permute-start | bytes 786440 | tf_op jit(solution)/shard_map/ppermute | solution.py:88
  9.4 34.3 %collective-permute-start.6 = (bf16[4,128,1,256]{3,1,0,2:T(8,128)(2,1)}, bf16[4,128,1,256]{3,1,0,2:T(8,128)(2,1)S(1)}, u32[]{:S(2)}, u32[]{:S(2)}) collective-permute-start(bf16[4,128,1,256]{3,1,0,2:T(8,128)(2,1)} %get-tuple-element.480), channel_id=1, source_target_pairs={{0,20},{4,16},{8,28},{12,24},{16,4},{20,0},{24,12},{28,8},{1,21},{... | collective-permute-start | bytes 786440 | tf_op jit(solution)/shard_map/ppermute | solution.py:88
  11.8 37.6 %collective-permute-start.7 = (bf16[4,128,1,256]{3,1,0,2:T(8,128)(2,1)}, bf16[4,128,1,256]{3,1,0,2:T(8,128)(2,1)S(1)}, u32[]{:S(2)}, u32[]{:S(2)}) collective-permute-start(bf16[4,128,1,256]{3,1,0,2:T(8,128)(2,1)} %get-tuple-element.479), channel_id=1, source_target_pairs={{0,24},{4,28},{8,16},{12,20},{16,8},{20,12},{24,0},{28,4},{1,25},{... | collective-permute-start | bytes 786440 | tf_op jit(solution)/shard_map/ppermute | solution.py:88
  22.5 31.1 %collective-permute-start.8 = (bf16[4,128,1,256]{3,1,0,2:T(8,128)(2,1)S(1)}, bf16[4,128,1,256]{3,1,0,2:T(8,128)(2,1)S(1)}, u32[]{:S(2)}, u32[]{:S(2)}) collective-permute-start(bf16[4,128,1,256]{3,1,0,2:T(8,128)(2,1)S(1)} %get-tuple-element.478), channel_id=1, source_target_pairs={{0,28},{4,24},{8,20},{12,16},{16,12},{20,8},{24,4},{28,0},{1,29},{... | collective-permute-start | bytes 786440 | tf_op jit(solution)/shard_map/ppermute | solution.py:88
  59.0 1.6 copy-start.1
  59.0 1.6 copy-start.2
  59.0 1.6 copy-start.3
  62.3 23.3 %collective-permute-start = (f32[128,2048]{1,0:T(8,128)S(1)}, f32[128,2048]{1,0:T(8,128)S(1)}, u32[]{:S(2)}, u32[]{:S(2)}) collective-permute-start(f32[128,2048]{1,0:T(8,128)S(1)} %get-tuple-element.630), channel_id=1, source_target_pairs={{0,4},{4,0},{8,12},{12,8},{16,20},{20,16},{24,28},{28,24},{1,5},{5... | collective-permute-start | bytes 3145736 | tf_op jit(solution)/shard_map/while/body/eval_jaxpr/ppermute | solution.py:25
  87.1 13.3 %collective-permute-start.1 = (bf16[128,2048]{1,0:T(8,128)(2,1)S(1)}, bf16[128,2048]{1,0:T(8,128)(2,1)S(1)}, u32[]{:S(2)}, u32[]{:S(2)}) collective-permute-start(bf16[128,2048]{1,0:T(8,128)(2,1)S(1)} %fusion.48), channel_id=1, source_target_pairs={{0,8},{4,12},{8,16},{12,20},{16,24},{20,28},{1,9},{5,13},{9,17},{1... | collective-permute-start | bytes 1572872 | tf_op jit(solution)/shard_map/while/body/eval_jaxpr/ppermute | solution.py:31
  117.1 21.6 %collective-permute-start = (f32[128,2048]{1,0:T(8,128)S(1)}, f32[128,2048]{1,0:T(8,128)S(1)}, u32[]{:S(2)}, u32[]{:S(2)}) collective-permute-start(f32[128,2048]{1,0:T(8,128)S(1)} %get-tuple-element.630), channel_id=1, source_target_pairs={{0,4},{4,0},{8,12},{12,8},{16,20},{20,16},{24,28},{28,24},{1,5},{5... | collective-permute-start | bytes 3145736 | tf_op jit(solution)/shard_map/while/body/eval_jaxpr/ppermute | solution.py:25
  140.3 11.3 %collective-permute-start.1 = (bf16[128,2048]{1,0:T(8,128)(2,1)S(1)}, bf16[128,2048]{1,0:T(8,128)(2,1)S(1)}, u32[]{:S(2)}, u32[]{:S(2)}) collective-permute-start(bf16[128,2048]{1,0:T(8,128)(2,1)S(1)} %fusion.48), channel_id=1, source_target_pairs={{0,8},{4,12},{8,16},{12,20},{16,24},{20,28},{1,9},{5,13},{9,17},{1... | collective-permute-start | bytes 1572872 | tf_op jit(solution)/shard_map/while/body/eval_jaxpr/ppermute | solution.py:31
  168.3 19.9 %collective-permute-start = (f32[128,2048]{1,0:T(8,128)S(1)}, f32[128,2048]{1,0:T(8,128)S(1)}, u32[]{:S(2)}, u32[]{:S(2)}) collective-permute-start(f32[128,2048]{1,0:T(8,128)S(1)} %get-tuple-element.630), channel_id=1, source_target_pairs={{0,4},{4,0},{8,12},{12,8},{16,20},{20,16},{24,28},{28,24},{1,5},{5... | collective-permute-start | bytes 3145736 | tf_op jit(solution)/shard_map/while/body/eval_jaxpr/ppermute | solution.py:25
  189.8 11.1 %collective-permute-start.1 = (bf16[128,2048]{1,0:T(8,128)(2,1)S(1)}, bf16[128,2048]{1,0:T(8,128)(2,1)S(1)}, u32[]{:S(2)}, u32[]{:S(2)}) collective-permute-start(bf16[128,2048]{1,0:T(8,128)(2,1)S(1)} %fusion.48), channel_id=1, source_target_pairs={{0,8},{4,12},{8,16},{12,20},{16,24},{20,28},{1,9},{5,13},{9,17},{1... | collective-permute-start | bytes 1572872 | tf_op jit(solution)/shard_map/while/body/eval_jaxpr/ppermute | solution.py:31
  217.6 17.9 %collective-permute-start = (f32[128,2048]{1,0:T(8,128)S(1)}, f32[128,2048]{1,0:T(8,128)S(1)}, u32[]{:S(2)}, u32[]{:S(2)}) collective-permute-start(f32[128,2048]{1,0:T(8,128)S(1)} %get-tuple-element.630), channel_id=1, source_target_pairs={{0,4},{4,0},{8,12},{12,8},{16,20},{20,16},{24,28},{28,24},{1,5},{5... | collective-permute-start | bytes 3145736 | tf_op jit(solution)/shard_map/while/body/eval_jaxpr/ppermute | solution.py:25
  237.0 11.1 %collective-permute-start.1 = (bf16[128,2048]{1,0:T(8,128)(2,1)S(1)}, bf16[128,2048]{1,0:T(8,128)(2,1)S(1)}, u32[]{:S(2)}, u32[]{:S(2)}) collective-permute-start(bf16[128,2048]{1,0:T(8,128)(2,1)S(1)} %fusion.48), channel_id=1, source_target_pairs={{0,8},{4,12},{8,16},{12,20},{16,24},{20,28},{1,9},{5,13},{9,17},{1... | collective-permute-start | bytes 1572872 | tf_op jit(solution)/shard_map/while/body/eval_jaxpr/ppermute | solution.py:31
  264.8 15.9 %collective-permute-start = (f32[128,2048]{1,0:T(8,128)S(1)}, f32[128,2048]{1,0:T(8,128)S(1)}, u32[]{:S(2)}, u32[]{:S(2)}) collective-permute-start(f32[128,2048]{1,0:T(8,128)S(1)} %get-tuple-element.630), channel_id=1, source_target_pairs={{0,4},{4,0},{8,12},{12,8},{16,20},{20,16},{24,28},{28,24},{1,5},{5... | collective-permute-start | bytes 3145736 | tf_op jit(solution)/shard_map/while/body/eval_jaxpr/ppermute | solution.py:25
  282.2 11.1 %collective-permute-start.1 = (bf16[128,2048]{1,0:T(8,128)(2,1)S(1)}, bf16[128,2048]{1,0:T(8,128)(2,1)S(1)}, u32[]{:S(2)}, u32[]{:S(2)}) collective-permute-start(bf16[128,2048]{1,0:T(8,128)(2,1)S(1)} %fusion.48), channel_id=1, source_target_pairs={{0,8},{4,12},{8,16},{12,20},{16,24},{20,28},{1,9},{5,13},{9,17},{1... | collective-permute-start | bytes 1572872 | tf_op jit(solution)/shard_map/while/body/eval_jaxpr/ppermute | solution.py:31
  294.9 14.9 %collective-permute-start = (f32[128,2048]{1,0:T(8,128)S(1)}, f32[128,2048]{1,0:T(8,128)S(1)}, u32[]{:S(2)}, u32[]{:S(2)}) collective-permute-start(f32[128,2048]{1,0:T(8,128)S(1)} %get-tuple-element.630), channel_id=1, source_target_pairs={{0,4},{4,0},{8,12},{12,8},{16,20},{20,16},{24,28},{28,24},{1,5},{5... | collective-permute-start | bytes 3145736 | tf_op jit(solution)/shard_map/while/body/eval_jaxpr/ppermute | solution.py:25
  311.3 24.9 %collective-permute-start.1 = (bf16[128,2048]{1,0:T(8,128)(2,1)S(1)}, bf16[128,2048]{1,0:T(8,128)(2,1)S(1)}, u32[]{:S(2)}, u32[]{:S(2)}) collective-permute-start(bf16[128,2048]{1,0:T(8,128)(2,1)S(1)} %fusion.48), channel_id=1, source_target_pairs={{0,8},{4,12},{8,16},{12,20},{16,24},{20,28},{1,9},{5,13},{9,17},{1... | collective-permute-start | bytes 1572872 | tf_op jit(solution)/shard_map/while/body/eval_jaxpr/ppermute | solution.py:31
  337.7 14.9 %collective-permute-start = (f32[128,2048]{1,0:T(8,128)S(1)}, f32[128,2048]{1,0:T(8,128)S(1)}, u32[]{:S(2)}, u32[]{:S(2)}) collective-permute-start(f32[128,2048]{1,0:T(8,128)S(1)} %get-tuple-element.630), channel_id=1, source_target_pairs={{0,4},{4,0},{8,12},{12,8},{16,20},{20,16},{24,28},{28,24},{1,5},{5... | collective-permute-start | bytes 3145736 | tf_op jit(solution)/shard_map/while/body/eval_jaxpr/ppermute | solution.py:25
  354.1 11.1 %collective-permute-start.1 = (bf16[128,2048]{1,0:T(8,128)(2,1)S(1)}, bf16[128,2048]{1,0:T(8,128)(2,1)S(1)}, u32[]{:S(2)}, u32[]{:S(2)}) collective-permute-start(bf16[128,2048]{1,0:T(8,128)(2,1)S(1)} %fusion.48), channel_id=1, source_target_pairs={{0,8},{4,12},{8,16},{12,20},{16,24},{20,28},{1,9},{5,13},{9,17},{1... | collective-permute-start | bytes 1572872 | tf_op jit(solution)/shard_map/while/body/eval_jaxpr/ppermute | solution.py:31
  366.4 23.4 %collective-permute-start.10 = (bf16[4,128,256]{2,1,0:T(8,128)(2,1)S(1)}, bf16[4,128,256]{2,1,0:T(8,128)(2,1)S(1)}, u32[]{:S(2)}, u32[]{:S(2)}) collective-permute-start(bf16[4,128,256]{2,1,0:T(8,128)(2,1)S(1)} %get-tuple-element.476), channel_id=1, source_target_pairs={{16,0},{20,4},{24,8},{28,12},{17,1},{21,5},{25,9},{29,13},{18,2},{... | collective-permute-start | bytes 786440 | tf_op jit(solution)/shard_map/ppermute | solution.py:31
  367.7 28.5 %collective-permute-start.11 = (bf16[4,128,256]{2,1,0:T(8,128)(2,1)S(1)}, bf16[4,128,256]{2,1,0:T(8,128)(2,1)S(1)}, u32[]{:S(2)}, u32[]{:S(2)}) collective-permute-start(bf16[4,128,256]{2,1,0:T(8,128)(2,1)S(1)} %get-tuple-element.475), channel_id=1, source_target_pairs={{8,0},{12,4},{16,8},{20,12},{24,16},{28,20},{9,1},{13,5},{17,9},{2... | collective-permute-start | bytes 786440 | tf_op jit(solution)/shard_map/ppermute | solution.py:31
  369.6 26.6 %collective-permute-start.9 = (bf16[4,128,256]{2,1,0:T(8,128)(2,1)S(1)}, bf16[4,128,256]{2,1,0:T(8,128)(2,1)S(1)}, u32[]{:S(2)}, u32[]{:S(2)}) collective-permute-start(bf16[4,128,256]{2,1,0:T(8,128)(2,1)S(1)} %get-tuple-element.477), channel_id=1, source_target_pairs={{24,0},{28,4},{25,1},{29,5},{26,2},{30,6},{27,3},{31,7}} | collective-permute-start | bytes 786440 | tf_op jit(solution)/shard_map/ppermute | solution.py:31
